TPU v7x, 256 devices: a whole 4x4x8 slice. The times are simulated.
256 devices in a mesh: dp: 8 (over y, x_hi), tok: 16 (over z, core), col: 2 (over x_lo).
Axes of the slice: x: 4 (x_hi: 2, x_lo: 2; x = x_hi * 2 + x_lo), y: 4, z: 8, core: 2. Of those that a mesh axis runs over, the one named last changes fastest.
Arguments:
- tokens: bfloat16 [8, 8192, 1024], P('dp', 'tok'), may hold values from -6 to 6
- ln_gain: bfloat16 [1024], replicated, may hold values from 0.099609375 to 1.8984375
- qkv_weight: bfloat16 [3, 1024, 512], P(None, None, 'col'), may hold values from -0.375 to 0.375
- out_weight: bfloat16 [512, 1024], P('col'), may hold values from -0.25 to 0.25
- readout_weight: bfloat16 [1024, 64], replicated, may hold values from -0.1875 to 0.1875
- conv_weight: bfloat16 [2, 64, 576], replicated, may hold values from -0.25 to 0.25
- head_weight: bfloat16 [2, 64], replicated, may hold values from -0.75 to 0.75
- holo_cot: float32 [8, 2, 32, 256], P('dp', None, 'tok', 'col'), may hold values from -1 to 1
Outputs:
- hologram: float32 [8, 2, 32, 256], P('dp', None, 'tok', 'col')
- conv_grad: float32 [2, 64, 576], replicated
- out_grad: float32 [512, 1024], P('col')
All inputs are finite; a program needn't handle non-finite values.
Results may differ from a plain program's by a relative error of at most 0.017.
The roundings to bfloat16 on the way count: a program that leaves them out, or rounds other values in their place, can miss the bound.
Values may be sent and summed in bfloat16 or wider, within the bound.
A program may use at most 128 MiB of HBM per device.

v0:
```python
import jax
import jax.numpy as jnp
from jax import lax
from jax.sharding import PartitionSpec as P

HEAD = 64
EPSILON = 1e-05


def extended(shard, sides, width):
    for axis, dim in sides:
        size, length = (lax.axis_size(axis), shard.shape[dim])
        up = [(i, (i + 1) % size) for i in range(size - 1)]
        down = [(j, i) for i, j in up]
        last = lax.slice_in_dim(shard, length - width, length, axis=dim)
        initial = lax.slice_in_dim(shard, 0, width, axis=dim)
        before = lax.ppermute(last, axis, up)
        after = lax.ppermute(initial, axis, down)
        shard = jnp.concatenate([before, shard, after], axis=dim)
    return shard


def joined_along(blocks, dim):
    shape = list(blocks.shape[1:])
    shape[dim] *= blocks.shape[0]
    return jnp.moveaxis(blocks, 0, dim).reshape(shape)


def copy_for_each(shard, axis):
    size = lax.axis_size(axis)
    return lax.all_to_all(
        jnp.broadcast_to(shard[None], (size, *shard.shape)), axis, 0, 0, tiled=True
    )


def gather_directly(shard, axis, dim):
    return joined_along(copy_for_each(shard, axis), dim)


def sent_together(arrays, axis, dim, along):
    ends, at = ([], 0)
    for a in arrays[:-1]:
        at += a.shape[along]
        ends.append(at)
    both = jnp.concatenate(arrays, axis=along)
    return tuple(jnp.split(lax.all_gather(both, axis, axis=dim, tiled=True), ends, axis=along))


def normalize(rows_in, ln_gain):
    values = rows_in.astype(jnp.float32)
    center = values - jnp.mean(values, axis=-1, keepdims=True)
    spread = jnp.mean(center * center, axis=-1, keepdims=True)
    return (center * lax.rsqrt(spread + EPSILON) * ln_gain.astype(jnp.float32)).astype(jnp.bfloat16)


def project(normed, weights_all):
    return tuple(
        (
            jnp.dot(normed, weights_all[member], preferred_element_type=jnp.float32).astype(
                jnp.bfloat16
            )
            for member in range(3)
        )
    )


def empty_state(queries):
    query_count = queries.shape[0]
    head_count = queries.shape[1] // HEAD
    return (
        jnp.zeros((query_count, head_count, HEAD), jnp.float32),
        jnp.full((head_count, query_count), -1e30, jnp.float32),
        jnp.zeros((head_count, query_count), jnp.float32),
    )


def absorb(queries, running, key_rows, value_rows):
    summed, row_top, row_total = running
    head_count = summed.shape[1]
    query_view = queries.reshape(queries.shape[0], head_count, HEAD)
    key_view = key_rows.reshape(key_rows.shape[0], head_count, HEAD)
    value_view = value_rows.reshape(value_rows.shape[0], head_count, HEAD)
    scores = jnp.einsum(
        "qhd,khd->hqk", query_view, key_view, preferred_element_type=jnp.float32
    ) * (1.0 / HEAD**0.5)
    new_top = jnp.maximum(row_top, jnp.max(scores, axis=-1))
    rescale = jnp.exp(row_top - new_top)
    raised = jnp.exp(scores - new_top[:, :, None])
    row_total = row_total * rescale + jnp.sum(raised, axis=-1)
    weighted = jnp.einsum(
        "hqk,khd->qhd", raised.astype(jnp.bfloat16), value_view, preferred_element_type=jnp.float32
    )
    summed = summed * jnp.transpose(rescale)[:, :, None] + weighted
    return (summed, new_top, row_total)


def absorb_keys(queries, running, arrived):
    key_rows, value_rows = arrived
    total_rows = key_rows.shape[0]
    block_rows = 512
    block_count = total_rows // block_rows

    def advance(turn_at, carried):
        key_block = lax.dynamic_slice_in_dim(key_rows, turn_at * block_rows, block_rows, 0)
        value_block = lax.dynamic_slice_in_dim(value_rows, turn_at * block_rows, block_rows, 0)
        return absorb(queries, carried, key_block, value_block)

    return lax.fori_loop(0, block_count, advance, running)


def finish(running):
    summed, row_top, row_total = running
    return (
        (summed / jnp.transpose(row_total)[:, :, None])
        .reshape(summed.shape[0], -1)
        .astype(jnp.bfloat16)
    )


def neighbourhood(padded, grid_rows, grid_cols):
    pieces = [
        padded[:, row_off : row_off + grid_rows, col_off : col_off + grid_cols]
        for row_off in range(3)
        for col_off in range(3)
    ]
    return jnp.concatenate(pieces, axis=0).reshape(9 * padded.shape[0], grid_rows * grid_cols)


def flipped(padded, grid_rows, grid_cols):
    pieces = [
        padded[:, 2 - row_off : 2 - row_off + grid_rows, 2 - col_off : 2 - col_off + grid_cols]
        for row_off in range(3)
        for col_off in range(3)
    ]
    return jnp.concatenate(pieces, axis=0).reshape(9 * padded.shape[0], grid_rows * grid_cols)


def transposed(weight):
    channels = weight.shape[0]
    return jnp.transpose(weight.reshape(channels, 9, channels), (2, 1, 0)).reshape(
        channels, 9 * channels
    )


def with_rims(field):
    return extended(field, (("tok", 1), ("col", 2)), 1)


def shards(
    tokens, ln_gain, qkv_weight, out_weight, readout_weight, conv_weight, head_weight, holo_cot
):
    frame_rows = tokens[0]
    cotangent = holo_cot[0]
    rows_dev = cotangent.shape[1]
    cols_dev = cotangent.shape[2]
    col_count = lax.axis_size("col")
    col_at = lax.axis_index("col")
    channels = conv_weight.shape[1]
    layer_count = conv_weight.shape[0]
    width = frame_rows.shape[1]
    own_rows = lax.dynamic_index_in_dim(
        frame_rows.reshape(rows_dev, col_count, cols_dev, width), col_at, 1, keepdims=False
    ).reshape(rows_dev * cols_dev, width)
    own_values = own_rows.astype(jnp.float32)
    readout_wide = readout_weight.astype(jnp.float32)
    readout_back = jnp.transpose(readout_wide)
    all_projections = lax.all_gather(qkv_weight, "col", axis=2, tiled=True)
    all_outputs = gather_directly(out_weight, "col", 0)
    normed = normalize(own_rows, ln_gain)
    queries, key_rows, value_rows = project(normed, all_projections)
    running = absorb_keys(
        queries, empty_state(queries), sent_together((key_rows, value_rows), ("tok", "col"), 0, 1)
    )
    context = finish(running)
    mixed = own_values + jnp.dot(context, all_outputs, preferred_element_type=jnp.float32)
    readout = jnp.dot(mixed, readout_wide, precision=lax.Precision.HIGHEST)
    hidden = jnp.transpose(readout.astype(jnp.bfloat16)).reshape(channels, rows_dev, cols_dev)
    inputs = []
    pre_acts = []
    for layer_at in range(layer_count):
        stacked = neighbourhood(with_rims(hidden), rows_dev, cols_dev)
        pre_act = jnp.dot(conv_weight[layer_at], stacked, preferred_element_type=jnp.float32)
        inputs.append(stacked)
        pre_acts.append(pre_act)
        hidden = jax.nn.silu(pre_act).astype(jnp.bfloat16).reshape(channels, rows_dev, cols_dev)
    hologram = jnp.dot(
        head_weight, hidden.reshape(channels, -1), preferred_element_type=jnp.float32
    )
    grad_hidden = jnp.dot(
        jnp.transpose(head_weight.astype(jnp.float32)),
        cotangent.reshape(cotangent.shape[0], -1),
        precision=lax.Precision.HIGHEST,
    ).astype(jnp.bfloat16)
    conv_terms = [None] * layer_count
    for layer_at in reversed(range(layer_count)):
        pre_act = pre_acts[layer_at]
        sigmoid_pre = jax.nn.sigmoid(pre_act)
        grad_pre = (
            grad_hidden.astype(jnp.float32) * sigmoid_pre * (1.0 + pre_act * (1.0 - sigmoid_pre))
        ).astype(jnp.bfloat16)
        conv_terms[layer_at] = lax.dot_general(
            grad_pre, inputs[layer_at], (((1,), (1,)), ((), ())), preferred_element_type=jnp.float32
        )
        padded = with_rims(grad_pre.reshape(channels, rows_dev, cols_dev))
        grad_hidden = jnp.dot(
            transposed(conv_weight[layer_at]),
            flipped(padded, rows_dev, cols_dev),
            preferred_element_type=jnp.float32,
        ).astype(jnp.bfloat16)
    conv_grad = lax.psum(jnp.stack(conv_terms), ("dp", "tok", "col"))
    shard_rows = out_weight.shape[0]
    small_term = lax.dot_general(
        context, grad_hidden, (((0,), (1,)), ((), ())), preferred_element_type=jnp.float32
    )
    grad_small = lax.psum(small_term, ("dp", "tok", "col"))
    own_small = lax.dynamic_slice_in_dim(grad_small, col_at * shard_rows, shard_rows, 0)
    out_grad = jnp.dot(own_small, readout_back, precision=lax.Precision.HIGHEST)
    return (hologram.reshape(1, cotangent.shape[0], rows_dev, cols_dev), conv_grad, out_grad)


def solution(mesh):
    in_specs = (
        P("dp", "tok", None),
        P(),
        P(None, None, "col"),
        P("col", None),
        P(),
        P(),
        P(),
        P("dp", None, "tok", "col"),
    )
    out_specs = (P("dp", None, "tok", "col"), P(), P("col", None))
    return jax.shard_map(shards, mesh=mesh, in_specs=in_specs, out_specs=out_specs, check_vma=False)
```

profile of v0, /device:TPU:1, one launch (start us, length us, event | category | flops | bytes accessed | tf_op | source)
XLA Modules:
  0.0 608.6 jit_solution(3435451693195484029)
XLA Ops:
  8.7 1.2 convert_reduce_fusion
  9.9 1.3 multiply_reduce_fusion
  11.2 1.3 multiply_convert_fusion
  12.6 50.8 %all-gather.3.cloned.1.call-done = bf16[3,1024,512]{2,1,0:T(8,128)(2,1)} async-done(((bf16[3,1024,256]{2,1,0:T(8,128)(2,1)}), bf16[3,1024,512]{2,1,0:T(8,128)(2,1)}) %all-gather.3.cloned.1.call-update) | async-done | bytes 3145744 | tf_op jit(solution)/shard_map/all_gather | solution.py:167
  63.4 1.7 convolution_convert_fusion.1
  65.1 1.7 convolution_convert_fusion.2
  67.7 1.1 broadcast_in_dim.28
  68.8 3.6 all-to-all-start
  72.5 1.1 dynamic-slice_convert_fusion
  73.6 1.7 convolution_convert_fusion
  75.4 107.3 %all-gather.5.cloned.1.call-done = bf16[8192,1024]{1,0:T(8,128)(2,1)} async-done(((bf16[256,1024]{1,0:T(8,128)(2,1)}), bf16[8192,1024]{1,0:T(8,128)(2,1)}) %all-gather.5.cloned.1.call-update) | async-done | bytes 16777232 | tf_op jit(solution)/shard_map/all_gather | solution.py:46
  182.7 11.3 %fusion.37 = (bf16[8192,512]{1,0:T(8,128)(2,1)}, bf16[8192,512]{1,0:T(8,128)(2,1)}) fusion(bf16[8192,1024]{1,0:T(8,128)(2,1)} %all-gather.5.cloned.1.call-done), kind=kLoop, calls=%fused_computation.157 | loop fusion | bytes 33554432 | tf_op jit(solution)/shard_map/split | solution.py:46
  194.1 67.4 %while.18 = (s32[]{:T(128)}, f32[256,8,64]{0,2,1:T(8,128)S(1)}, f32[8,256]{1,0:T(8,128)S(1)}, f32[8,256]{1,0:T(8,128)S(1)}, bf16[8192,512]{1,0:T(8,128)(2,1)}, /...) while((s32[]{:T(128)}, f32[256,8,64]{0,2,1:T(8,128)S(1)}, ...), condition=%wide.region_5.6_spmd.clone, body=%wide.region_2.5_spmd.clone.sunk | while | flops 277229568 | bytes 19267760 | solution.py:108
  194.1 1.3 constant_dynamic-slice_fusion.3
  196.6 1.0 fusion.84
  198.3 1.3 constant_dynamic-slice_fusion.3
  202.5 1.3 constant_dynamic-slice_fusion.3
  205.0 0.9 fusion.84
  206.7 1.3 constant_dynamic-slice_fusion.3
  209.2 1.0 fusion.84
  210.9 1.3 constant_dynamic-slice_fusion.3
  215.1 1.3 constant_dynamic-slice_fusion.3
  217.6 0.9 fusion.84
  219.3 1.3 constant_dynamic-slice_fusion.3
  221.9 1.0 fusion.84
  223.6 1.3 constant_dynamic-slice_fusion.3
  227.8 1.3 constant_dynamic-slice_fusion.3
  232.0 1.3 constant_dynamic-slice_fusion.3
  234.5 1.0 fusion.84
  236.2 1.3 constant_dynamic-slice_fusion.3
  240.4 1.3 constant_dynamic-slice_fusion.3
  244.6 1.3 constant_dynamic-slice_fusion.3
  247.2 1.0 fusion.84
  248.9 1.3 constant_dynamic-slice_fusion.3
  253.1 1.3 constant_dynamic-slice_fusion.3
  257.3 1.3 constant_dynamic-slice_fusion.3
  259.8 1.0 fusion.84
  261.6 1.7 convolution_add_fusion
  264.1 5.3 collective-permute-start
  269.4 1.9 collective-permute-start.1
  271.3 3.3 collective-permute-done.1
  274.8 2.0 collective-permute-start.2
  276.9 1.3 collective-permute-start.3
  278.8 3.1 collective-permute-done.3
  283.1 4.1 collective-permute-start.4
  287.2 1.9 collective-permute-start.5
  289.1 3.3 collective-permute-done.5
  292.6 1.3 collective-permute-start.6
  293.9 1.3 collective-permute-start.7
  295.9 3.1 collective-permute-done.7
  300.4 4.1 collective-permute-start.8
  304.5 1.9 collective-permute-start.9
  307.0 2.7 collective-permute-done.9
  309.9 1.3 collective-permute-start.10
  311.4 4.2 collective-permute-start.11
  317.9 3.9 collective-permute-start.12
  321.9 1.9 collective-permute-start.13
  324.0 3.3 collective-permute-done.13
  327.6 1.3 collective-permute-start.14
  329.6 4.0 collective-permute-start.15
  335.8 1.2 fusion.16
  337.7 260.2 %all-reduce.3.cloned.1.call-done = (f32[2,64,576]{2,1,0:T(8,128)}, f32[512,64]{1,0:T(8,128)}) async-done(((f32[2,64,576]{2,1,0:T(8,128)}, f32[512,64]{1,0:T(8,128)}), (f32[2,64,576]{2,1,0:T(8,128)}, f32[512,64]{1,0:T(8,128)})) %all-reduce.3.cloned.1.call-update) | async-done | bytes 426000 | tf_op jit(solution)/shard_map/psum | solution.py:210
  597.9 2.4 fusion.27
  600.3 1.7 copy.147
  (233 shorter events, 53.1 us)
Async XLA Ops:
  7.2 256.1 %copy-start = (bf16[1024,64]{0,1:T(8,128)(2,1)S(1)}, bf16[1024,64]{0,1:T(8,128)(2,1)}, u32[]{:S(2)}) copy-start(bf16[1024,64]{0,1:T(8,128)(2,1)} %param.14) | copy-start | bytes 393220
  7.2 56.2 %all-gather.3.cloned.1.call-start = ((), (), s32[]{:S(2)}) async-start(), calls=%async_computation.1 | async-start | bytes 4718592 | tf_op jit(solution)/shard_map/all_gather | solution.py:167
  7.9 59.8 %copy-start.2 = (bf16[256,1024]{1,0:T(8,128)(2,1)S(1)}, bf16[256,1024]{1,0:T(8,128)(2,1)}, u32[]{:S(2)}) copy-start(bf16[256,1024]{1,0:T(8,128)(2,1)} %param.13) | copy-start | bytes 1572868
  7.9 174.8 %all-gather.5.cloned.1.call-start = ((), (), s32[]{:S(2)}) async-start(), calls=%async_computation.2 | async-start | bytes 17301504 | tf_op jit(solution)/shard_map/all_gather | solution.py:46
  65.0 7.5 %copy-start.1 = (bf16[1,512,1024]{2,1,0:T(8,128)(2,1)S(1)}, bf16[1,512,1024]{2,1,0:T(8,128)(2,1)}, u32[]{:S(2)}) copy-start(bf16[1,512,1024]{2,1,0:T(8,128)(2,1)} %param.10) | copy-start | bytes 3145732
  68.8 192.7 %all-to-all-start = ((bf16[2,256,1024]{2,1,0:T(8,128)(2,1)}), bf16[2,256,1024]{2,1,0:T(8,128)(2,1)S(1)}, u32[]{:S(2)}, u32[]{:S(2)}) async-start(bf16[2,256,1024]{2,1,0:T(8,128)(2,1)} %broadcast_in_dim.28), calls=%async_computation | async-start | bytes 2097152 | tf_op jit(solution)/shard_map/all_to_all | solution.py:31
  72.4 525.5 %all-reduce.3.cloned.1.call-start = ((), (), s32[]{:S(2)}) async-start(), calls=%async_computation.3 | async-start | bytes 1179648 | tf_op jit(solution)/shard_map/psum | solution.py:210
  261.5 21.3 %copy-start.3 = (bf16[2,64,576]{2,1,0:T(8,128)(2,1)S(1)}, bf16[2,64,576]{2,1,0:T(8,128)(2,1)}, u32[]{:S(2)}) copy-start(bf16[2,64,576]{2,1,0:T(8,128)(2,1)} %param.15) | copy-start | bytes 442372
  261.6 38.5 %copy-start.4 = (f32[1,2,2,128]{3,2,1,0:T(2,128)S(1)}, f32[1,2,2,128]{3,2,1,0:T(2,128)}, u32[]{:S(2)}) copy-start(f32[1,2,2,128]{3,2,1,0:T(2,128)} %param.17) | copy-start | bytes 6148
  261.6 38.5 %copy-start.5 = (bf16[2,64]{1,0:T(2,128)(2,1)S(1)}, bf16[2,64]{1,0:T(2,128)(2,1)}, u32[]{:S(2)}) copy-start(bf16[2,64]{1,0:T(2,128)(2,1)} %param.16) | copy-start | bytes 772
  264.1 7.3 %collective-permute-start = (bf16[64,1,128]{2,1,0:T(2,128)(2,1)S(1)}, bf16[64,1,128]{2,1,0:T(2,128)(2,1)S(1)}, u32[]{:S(2)}, u32[]{:S(2)}) collective-permute-start(bf16[64,1,128]{2,1,0:T(2,128)(2,1)S(1)} %get-tuple-element.240), channel_id=1, source_target_pairs={{0,2},{2,4},{4,6},{6,8},{8,10},{10,12},{12,14},{14,16},{16,18},{18... | collective-permute-start | bytes 49160 | tf_op jit(solution)/shard_map/ppermute | solution.py:17
  269.4 5.2 collective-permute-start.1
  274.8 3.3 collective-permute-start.2
  276.9 5.0 collective-permute-start.3
  283.1 6.0 collective-permute-start.4
  287.2 5.2 collective-permute-start.5
  292.6 2.6 collective-permute-start.6
  293.9 5.0 collective-permute-start.7
  300.4 6.6 %collective-permute-start.8 = (bf16[64,1,128]{2,1,0:T(2,128)(2,1)S(1)}, bf16[64,1,128]{2,1,0:T(2,128)(2,1)S(1)}, u32[]{:S(2)}, u32[]{:S(2)}) collective-permute-start(bf16[64,1,128]{2,1,0:T(2,128)(2,1)S(1)} %get-tuple-element.236), channel_id=1, source_target_pairs={{0,2},{2,4},{4,6},{6,8},{8,10},{10,12},{12,14},{14,16},{16,18},{18... | collective-permute-start | bytes 49160 | tf_op jit(solution)/shard_map/ppermute | solution.py:17
  304.5 5.2 collective-permute-start.9
  309.9 5.7 collective-permute-start.10
  311.4 5.3 collective-permute-start.11
  317.9 6.1 %collective-permute-start.12 = (bf16[64,1,128]{2,1,0:T(2,128)(2,1)S(1)}, bf16[64,1,128]{2,1,0:T(2,128)(2,1)S(1)}, u32[]{:S(2)}, u32[]{:S(2)}) collective-permute-start(bf16[64,1,128]{2,1,0:T(2,128)(2,1)S(1)} %get-tuple-element.234), channel_id=1, source_target_pairs={{0,2},{2,4},{4,6},{6,8},{8,10},{10,12},{12,14},{14,16},{16,18},{18... | collective-permute-start | bytes 49160 | tf_op jit(solution)/shard_map/ppermute | solution.py:17
  321.9 5.4 collective-permute-start.13
  327.6 6.0 collective-permute-start.14
  329.6 5.3 collective-permute-start.15
Sparse Core Ops, SparseCore 0:
  9.8 53.5 all-gather.2
  67.8 114.8 all-gather.4
  337.1 260.7 all-reduce.2
where the time goes:
time: 610 us; the launch traced here: 609 us
  waiting for transfers between devices  439 us (72%)
  starting transfers between devices  45.4 us (7%)
  local copies, waits for them, and re-layouts  43.8 us (7%)
  matrix products  39.9 us (7%)
  other arithmetic  25 us (4%)
  between operations  14.5 us (2%)
    psum x1, waiting for transfers between devices, shards(): conv_grad = lax.psum(jnp.stack(conv_terms), ('dp', 'tok', 'col'))  260 us
    all_gather x1, waiting for transfers between devices, sent_together(): lax.all_gather(both, axis, axis=dim, tiled=True)  107 us
    all_gather x1, waiting for transfers between devices, shards(): all_projections = lax.all_gather(qkv_weight, 'col', axis=2, tiled=True)  50.8 us
    ppermute x8, starting transfers between devices, extended(): before = lax.ppermute(last, axis, up)  28.8 us
    dynamic_slice x32, local copies, waits for them, and re-layouts, advance(): lax.dynamic_slice_in_dim(value_rows, turn_at * block_rows, block_rows, 0)  23.8 us
    ppermute x8, waiting for transfers between devices, extended(): after = lax.ppermute(initial, axis, down)  18.7 us
    dot_general x16, matrix products, absorb(): jnp.einsum('hqk,khd->qhd', raised.astype(jnp.bfloat16), value_view, prefe...  15.2 us
    ppermute x8, starting transfers between devices, extended(): after = lax.ppermute(initial, axis, down)  12.9 us
  transfers between devices with their start and end apart: 20, of which 11 were waited for; matrix products, arithmetic and copies ran while one was open for 15% of the time, Pallas kernels for 0%

commit v1 on v0

--- a/solution.py
+++ b/solution.py
@@ -207,7 +207,8 @@
             flipped(padded, rows_dev, cols_dev),
             preferred_element_type=jnp.float32,
         ).astype(jnp.bfloat16)
-    conv_grad = lax.psum(jnp.stack(conv_terms), ("dp", "tok", "col"))
+    half = lax.psum(jnp.stack(conv_terms), "dp")
+    conv_grad = lax.psum(half, ("tok", "col"))
     shard_rows = out_weight.shape[0]
     small_term = lax.dot_general(
         context, grad_hidden, (((0,), (1,)), ((), ())), preferred_element_type=jnp.float32

time: 610 us -> 916 us (1.50)
  waiting for transfers between devices: 439 us -> 745 us
    psum x1 -> x3, waiting for transfers between devices: 260 us -> 566 us  [the longest x1 261 us: shards(): grad_small = lax.psum(small_term, ('dp', 'tok', 'col'))]
  transfers between devices with their start and end apart: 20 -> 22, of which waited for: 11 -> 13; matrix products, arithmetic and copies ran while one was open for 15% -> 10% of each run, Pallas kernels for 0% -> 0%
where the time goes in v1:
time: 916 us; the launch traced here: 915 us
  waiting for transfers between devices  745 us (81%)
  starting transfers between devices  45.5 us (5%)
  local copies, waits for them, and re-layouts  43.7 us (5%)
  matrix products  39.9 us (4%)
  other arithmetic  25 us (3%)
  between operations  14.6 us (2%)
    psum x1, waiting for transfers between devices, shards(): grad_small = lax.psum(small_term, ('dp', 'tok', 'col'))  261 us
    psum x1, waiting for transfers between devices, shards(): conv_grad = lax.psum(half, ('tok', 'col'))  221 us
    all_gather x1, waiting for transfers between devices, sent_together(): lax.all_gather(both, axis, axis=dim, tiled=True)  107 us
    psum x1, waiting for transfers between devices, shards(): half = lax.psum(jnp.stack(conv_terms), 'dp')  84.5 us
    all_gather x1, waiting for transfers between devices, shards(): all_projections = lax.all_gather(qkv_weight, 'col', axis=2, tiled=True)  50.8 us
    ppermute x8, starting transfers between devices, extended(): before = lax.ppermute(last, axis, up)  28.8 us
    dynamic_slice x32, local copies, waits for them, and re-layouts, advance(): lax.dynamic_slice_in_dim(value_rows, turn_at * block_rows, block_rows, 0)  23.8 us
    ppermute x8, waiting for transfers between devices, extended(): after = lax.ppermute(initial, axis, down)  18.7 us
  transfers between devices with their start and end apart: 22, of which 13 were waited for; matrix products, arithmetic and copies ran while one was open for 10% of the time, Pallas kernels for 0%

profile of v1, /device:TPU:1, one launch (start us, length us, event | category | flops | bytes accessed | tf_op | source)
XLA Modules:
  0.0 914.8 jit_solution(4305527492648513184)
XLA Ops:
  8.7 1.2 convert_reduce_fusion
  9.9 1.3 multiply_reduce_fusion
  11.2 1.3 multiply_convert_fusion
  12.6 50.8 %all-gather.3.cloned.1.call-done = bf16[3,1024,512]{2,1,0:T(8,128)(2,1)} async-done(((bf16[3,1024,256]{2,1,0:T(8,128)(2,1)}), bf16[3,1024,512]{2,1,0:T(8,128)(2,1)}) %all-gather.3.cloned.1.call-update) | async-done | bytes 3145744 | tf_op jit(solution)/shard_map/all_gather | solution.py:167
  63.4 1.7 convolution_convert_fusion.1
  65.1 1.7 convolution_convert_fusion.2
  67.7 1.1 broadcast_in_dim.28
  68.8 3.6 all-to-all-start
  72.5 1.1 dynamic-slice_convert_fusion
  73.6 1.7 convolution_convert_fusion
  75.4 107.3 %all-gather.5.cloned.1.call-done = bf16[8192,1024]{1,0:T(8,128)(2,1)} async-done(((bf16[256,1024]{1,0:T(8,128)(2,1)}), bf16[8192,1024]{1,0:T(8,128)(2,1)}) %all-gather.5.cloned.1.call-update) | async-done | bytes 16777232 | tf_op jit(solution)/shard_map/all_gather | solution.py:46
  182.7 11.3 %fusion.37 = (bf16[8192,512]{1,0:T(8,128)(2,1)}, bf16[8192,512]{1,0:T(8,128)(2,1)}) fusion(bf16[8192,1024]{1,0:T(8,128)(2,1)} %all-gather.5.cloned.1.call-done), kind=kLoop, calls=%fused_computation.157 | loop fusion | bytes 33554432 | tf_op jit(solution)/shard_map/split | solution.py:46
  194.0 67.4 %while.18 = (s32[]{:T(128)}, f32[256,8,64]{0,2,1:T(8,128)S(1)}, f32[8,256]{1,0:T(8,128)S(1)}, f32[8,256]{1,0:T(8,128)S(1)}, bf16[8192,512]{1,0:T(8,128)(2,1)}, /...) while((s32[]{:T(128)}, f32[256,8,64]{0,2,1:T(8,128)S(1)}, ...), condition=%wide.region_5.6_spmd.clone, body=%wide.region_2.5_spmd.clone.sunk | while | flops 277229568 | bytes 19267760 | solution.py:108
  194.0 1.3 constant_dynamic-slice_fusion.3
  196.5 1.0 fusion.84
  198.3 1.3 constant_dynamic-slice_fusion.3
  202.5 1.3 constant_dynamic-slice_fusion.3
  206.7 1.3 constant_dynamic-slice_fusion.3
  209.2 1.0 fusion.84
  210.9 1.3 constant_dynamic-slice_fusion.3
  215.1 1.3 constant_dynamic-slice_fusion.3
  219.3 1.3 constant_dynamic-slice_fusion.3
  221.8 1.0 fusion.84
  223.5 1.3 constant_dynamic-slice_fusion.3
  227.8 1.3 constant_dynamic-slice_fusion.3
  232.0 1.3 constant_dynamic-slice_fusion.3
  234.5 1.0 fusion.84
  236.2 1.3 constant_dynamic-slice_fusion.3
  240.4 1.3 constant_dynamic-slice_fusion.3
  244.6 1.3 constant_dynamic-slice_fusion.3
  247.1 1.0 fusion.84
  248.8 1.3 constant_dynamic-slice_fusion.3
  253.1 1.3 constant_dynamic-slice_fusion.3
  257.3 1.3 constant_dynamic-slice_fusion.3
  259.8 1.0 fusion.84
  261.6 1.7 convolution_add_fusion
  264.0 5.3 collective-permute-start
  269.4 1.9 collective-permute-start.1
  271.3 3.3 collective-permute-done.1
  274.8 2.0 collective-permute-start.2
  276.8 1.3 collective-permute-start.3
  278.8 3.1 collective-permute-done.3
  283.1 4.1 collective-permute-start.4
  287.1 1.9 collective-permute-start.5
  289.1 3.3 collective-permute-done.5
  292.6 1.3 collective-permute-start.6
  293.9 1.3 collective-permute-start.7
  295.9 3.1 collective-permute-done.7
  300.4 4.1 collective-permute-start.8
  304.4 1.9 collective-permute-start.9
  307.0 2.7 collective-permute-done.9
  309.9 1.3 collective-permute-start.10
  311.4 4.2 collective-permute-start.11
  317.9 3.9 collective-permute-start.12
  321.9 1.9 collective-permute-start.13
  324.0 3.3 collective-permute-done.13
  327.5 1.3 collective-permute-start.14
  329.7 4.0 collective-permute-start.15
  335.8 1.2 fusion.16
  337.1 84.5 %all-reduce.4.cloned.1.call-done = f32[2,64,576]{2,1,0:T(8,128)} async-done(((f32[2,64,576]{2,1,0:T(8,128)}), f32[2,64,576]{2,1,0:T(8,128)}) %all-reduce.4.cloned.1.call-update) | async-done | bytes 294928 | tf_op jit(solution)/shard_map/psum | solution.py:210
  422.4 260.9 %all-reduce.8.cloned.1.call-done = f32[512,64]{1,0:T(8,128)} async-done(((f32[512,64]{1,0:T(8,128)}), f32[512,64]{1,0:T(8,128)}) %all-reduce.8.cloned.1.call-update) | async-done | bytes 131088 | tf_op jit(solution)/shard_map/psum | solution.py:216
  683.3 2.4 fusion.27
  685.7 220.8 %all-reduce.6.cloned.1.call-done = f32[2,64,576]{2,1,0:T(8,128)} async-done(((f32[2,64,576]{2,1,0:T(8,128)}), f32[2,64,576]{2,1,0:T(8,128)}) %all-reduce.6.cloned.1.call-update) | async-done | bytes 294928 | tf_op jit(solution)/shard_map/psum | solution.py:211
  906.5 1.7 copy.148
  (239 shorter events, 55.2 us)
Async XLA Ops:
  7.2 256.1 %copy-start = (bf16[1024,64]{0,1:T(8,128)(2,1)S(1)}, bf16[1024,64]{0,1:T(8,128)(2,1)}, u32[]{:S(2)}) copy-start(bf16[1024,64]{0,1:T(8,128)(2,1)} %param.14) | copy-start | bytes 393220
  7.2 56.2 %all-gather.3.cloned.1.call-start = ((), (), s32[]{:S(2)}) async-start(), calls=%async_computation.1 | async-start | bytes 4718592 | tf_op jit(solution)/shard_map/all_gather | solution.py:167
  7.9 59.8 %copy-start.2 = (bf16[256,1024]{1,0:T(8,128)(2,1)S(1)}, bf16[256,1024]{1,0:T(8,128)(2,1)}, u32[]{:S(2)}) copy-start(bf16[256,1024]{1,0:T(8,128)(2,1)} %param.13) | copy-start | bytes 1572868
  7.9 174.8 %all-gather.5.cloned.1.call-start = ((), (), s32[]{:S(2)}) async-start(), calls=%async_computation.2 | async-start | bytes 17301504 | tf_op jit(solution)/shard_map/all_gather | solution.py:46
  65.0 7.4 copy-start.1
  68.8 192.7 %all-to-all-start = ((bf16[2,256,1024]{2,1,0:T(8,128)(2,1)}), bf16[2,256,1024]{2,1,0:T(8,128)(2,1)S(1)}, u32[]{:S(2)}, u32[]{:S(2)}) async-start(bf16[2,256,1024]{2,1,0:T(8,128)(2,1)} %broadcast_in_dim.28), calls=%async_computation | async-start | bytes 2097152 | tf_op jit(solution)/shard_map/all_to_all | solution.py:31
  72.4 349.2 %all-reduce.4.cloned.1.call-start = ((), (), s32[]{:S(2)}) async-start(), calls=%async_computation.3 | async-start | bytes 655360 | tf_op jit(solution)/shard_map/psum | solution.py:210
  261.5 21.3 %copy-start.3 = (bf16[2,64,576]{2,1,0:T(8,128)(2,1)S(1)}, bf16[2,64,576]{2,1,0:T(8,128)(2,1)}, u32[]{:S(2)}) copy-start(bf16[2,64,576]{2,1,0:T(8,128)(2,1)} %param.15) | copy-start | bytes 442372
  261.6 38.5 %copy-start.4 = (f32[1,2,2,128]{3,2,1,0:T(2,128)S(1)}, f32[1,2,2,128]{3,2,1,0:T(2,128)}, u32[]{:S(2)}) copy-start(f32[1,2,2,128]{3,2,1,0:T(2,128)} %param.17) | copy-start | bytes 6148
  261.6 38.5 %copy-start.5 = (bf16[2,64]{1,0:T(2,128)(2,1)S(1)}, bf16[2,64]{1,0:T(2,128)(2,1)}, u32[]{:S(2)}) copy-start(bf16[2,64]{1,0:T(2,128)(2,1)} %param.16) | copy-start | bytes 772
  264.0 7.3 collective-permute-start
  269.4 5.2 collective-permute-start.1
  274.8 3.3 collective-permute-start.2
  276.8 5.0 collective-permute-start.3
  283.1 6.0 collective-permute-start.4
  287.1 5.2 collective-permute-start.5
  292.6 2.6 collective-permute-start.6
  293.9 5.0 collective-permute-start.7
  300.4 6.6 collective-permute-start.8
  304.4 5.2 collective-permute-start.9
  309.9 5.7 collective-permute-start.10
  311.4 5.3 collective-permute-start.11
  317.9 6.1 collective-permute-start.12
  321.9 5.4 collective-permute-start.13
  327.5 6.1 collective-permute-start.14
  329.6 353.7 %all-reduce.8.cloned.1.call-start = ((), (), s32[]{:S(2)}) async-start(), calls=%async_computation.5 | async-start | bytes 524288 | tf_op jit(solution)/shard_map/psum | solution.py:216
  329.7 5.3 collective-permute-start.15
  337.1 569.5 %all-reduce.6.cloned.1.call-start = ((), (), s32[]{:S(2)}) async-start(), calls=%async_computation.4 | async-start | bytes 655360 | tf_op jit(solution)/shard_map/psum | solution.py:211
Sparse Core Ops, SparseCore 0:
  9.8 53.5 all-gather.2
  67.8 114.8 all-gather.4
  329.7 91.8 all-reduce.3
  427.5 255.7 all-reduce.7
  685.8 220.7 all-reduce.5
